TPU v7x, 32 devices: a whole 2x2x4 slice. The times are simulated.
32 devices in a mesh: grp: 2 (over y), row: 4 (over z), col: 2 (over x), cls: 2 (over core).
Axes of the slice: x: 2, y: 2, z: 4, core: 2. Of those that a mesh axis runs over, the one named last changes fastest.
Arguments:
- unary_scores: int32 [32, 16, 256], P('cls', ('grp', 'row'), 'col'), parts along dimension 1, may hold values from -256 to 256
- confidence: float32 [16, 256], P(('grp', 'row'), 'col'), parts along dimension 0, may hold values from 0.5 to 64
- features: bfloat16 [16, 256, 256], P(('grp', 'row'), 'col'), parts along dimension 0, may hold values from -12 to 12
- compat_table: int32 [32, 32], replicated, may hold values from 0 to 7
Outputs:
- belief: bfloat16 [32, 16, 256], P('cls', ('grp', 'row'), 'col'), parts along dimension 1
There are 2 independent parts, one for each index of `grp`. A program takes and returns all parts, laid end to end along the dimension named above; an argument that names none is the same for every part. Nothing has to cross between parts.
All inputs are finite; a program needn't handle non-finite values.
Results may differ from a plain program's by a relative error of at most 0.0021.
Values may be sent and summed in bfloat16 or wider, within the bound.
A program may use at most 64 MiB of HBM per device.

v0:
```python
import jax
import jax.numpy as jnp
from jax import lax
from jax.sharding import PartitionSpec as P

LIVE = 21


unit_scale = 1.0 / 64.0
masked_low = -1e30
key_block = 1024


def class_softmax(logits, live_mask):
    class_top = jnp.max(jnp.where(live_mask, logits, masked_low), axis=0)
    raised = jnp.where(live_mask, jnp.exp(logits - class_top[None]), 0.0)
    return raised / jnp.sum(raised, axis=0)[None]


def make_fold(query_feats, query_norm, query_ids, key_ids, feat_depth):

    def add_block(running, key_piece, beliefs, key_start):
        key_count = key_piece.shape[1]
        scores = jnp.dot(query_feats, key_piece, preferred_element_type=jnp.float32)
        key_norm = jnp.sum(jnp.square(key_piece.astype(jnp.float32)), axis=0)
        spread = (query_norm[:, None] + key_norm[None, :] - 2.0 * scores) * (2.0 / feat_depth)
        same_pixel = query_ids[:, None] == key_ids(key_start, key_count)[None, :]
        kernel = jnp.where(same_pixel, 0.0, jnp.exp(4.0 - spread)).astype(jnp.bfloat16)
        return running + lax.dot_general(
            beliefs, kernel, (((1,), (1,)), ((), ())), preferred_element_type=jnp.float32
        )

    def fold_keys(running, pieces, key_start):
        key_piece, beliefs = pieces
        key_count = key_piece.shape[1]
        if key_count > key_block and key_count % key_block == 0:

            def block_step(block_index, running_sum):
                block_start = block_index * key_block
                return add_block(
                    running_sum,
                    lax.dynamic_slice_in_dim(key_piece, block_start, key_block, 1),
                    lax.dynamic_slice_in_dim(beliefs, block_start, key_block, 1),
                    key_start + block_start,
                )

            return lax.fori_loop(0, key_count // key_block, block_step, running)
        return add_block(running, key_piece, beliefs, key_start)

    return fold_keys


def body(unary_scores, confidence, features, compat_table):
    class_share, row_count, col_count = unary_scores.shape
    feat_depth = features.shape[2]
    cls_count = lax.axis_size("cls")
    col_groups = lax.axis_size("col")
    cls_index = lax.axis_index("cls")
    row_index = lax.axis_index("row")
    col_index = lax.axis_index("col")
    full_width = col_count * col_groups
    pixels = row_count * col_count
    half_cols = col_count // cls_count
    keys_local = row_count * half_cols
    whole_unary = lax.all_gather(unary_scores, "cls", axis=0, tiled=True)
    classes = whole_unary.shape[0]
    logits0 = confidence[None] * (whole_unary.astype(jnp.float32) * unit_scale)
    live_all = (lax.iota(jnp.int32, classes) < LIVE)[:, None, None]
    belief0 = class_softmax(logits0, live_all).astype(jnp.bfloat16)
    offset = cls_index * half_cols
    key_belief = lax.dynamic_slice_in_dim(belief0, offset, half_cols, 2).reshape(
        classes, keys_local
    )
    key_feats = (
        lax.dynamic_slice_in_dim(features, offset, half_cols, 1).reshape(keys_local, feat_depth).T
    )

    def spread_ids(key_start, key_count):
        key_place = key_start + lax.iota(jnp.int32, key_count)
        key_owner = key_place // keys_local
        within = key_place % keys_local
        global_row = key_owner // col_groups * row_count + within // half_cols
        global_col = key_owner % col_groups * col_count + offset + within % half_cols
        return global_row * full_width + global_col

    query_feats = features.reshape(pixels, feat_depth)
    query_norm = jnp.sum(jnp.square(query_feats.astype(jnp.float32)), axis=1)
    local_ids = lax.iota(jnp.int32, pixels)
    query_ids = (
        (row_index * row_count + local_ids // col_count) * full_width
        + col_index * col_count
        + local_ids % col_count
    )
    fold_own = make_fold(query_feats, query_norm, query_ids, spread_ids, feat_depth)
    zero_start = jnp.zeros((classes, pixels), jnp.float32)
    band_feats, band_belief = (
        lax.all_gather(key_feats, "col", axis=1, tiled=True),
        lax.all_gather(key_belief, "col", axis=1, tiled=True),
    )
    message = fold_own(
        zero_start,
        (
            lax.all_gather(band_feats, "row", axis=1, tiled=True),
            lax.all_gather(band_belief, "row", axis=1, tiled=True),
        ),
        jnp.int32(0),
    )
    message = message / (2.0 * pixels)
    potts_weight = compat_table.astype(jnp.float32) * (1.0 - jnp.eye(classes, dtype=jnp.float32))
    partial_value = jnp.dot(potts_weight, message, precision=lax.Precision.HIGHEST)
    pairwise = lax.psum(partial_value, "cls")
    logits1 = logits0.reshape(classes, pixels) - pairwise
    belief1 = class_softmax(logits1, live_all.reshape(classes, 1))
    own_belief = lax.dynamic_slice_in_dim(belief1, cls_index * class_share, class_share, 0)
    return own_belief.astype(jnp.bfloat16).reshape(class_share, row_count, col_count)


def solution(mesh):
    in_specs = (
        P("cls", ("grp", "row"), "col"),
        P(("grp", "row"), "col"),
        P(("grp", "row"), "col", None),
        P(),
    )
    out_specs = P("cls", ("grp", "row"), "col")
    return jax.shard_map(body, mesh=mesh, in_specs=in_specs, out_specs=out_specs, check_vma=False)
```

profile of v0, /device:TPU:0, one launch (start us, length us, event | category | flops | bytes accessed | tf_op | source)
XLA Modules:
  0.0 48.1 jit_solution(6375300446395197448)
XLA Ops:
  0.0 0.0 copy-start.2
  0.0 2.2 %all_gather.15 = s32[32,2,128]{2,1,0:T(2,128)S(1)} all-gather(s32[16,2,128]{2,1,0:T(2,128)} %param.4), channel_id=1, replica_groups=mesh['grp'=2,'row'=4,'col'=2,'cls'=2] {'cls'}, dimensions={0}, use_global_device_ids=true | all-gather | bytes 49152 | tf_op jit(solution)/shard_map/all_gather | solution.py:65
  2.2 0.0 copy-done.2
  2.2 0.1 select_reduce_fusion.1
  2.3 0.0 copy-start
  2.3 0.1 fusion.67
  2.4 0.1 constant_dynamic-slice_fusion.1
  2.5 0.1 fusion.19
  2.6 0.1 reshape.136
  2.7 5.1 %all_gather.16 = bf16[32,256]{1,0:T(8,128)(2,1)S(1)} all-gather(bf16[32,128]{1,0:T(8,128)(2,1)S(1)} %reshape.136), channel_id=1, replica_groups=mesh['grp'=2,'row'=4,'col'=2,'cls'=2] {'col'}, dimensions={1}, use_global_device_ids=true | all-gather | bytes 24576 | tf_op jit(solution)/shard_map/all_gather | solution.py:98
  7.8 14.0 %all_gather.17 = bf16[32,1024]{1,0:T(8,128)(2,1)S(1)} all-gather(bf16[32,256]{1,0:T(8,128)(2,1)S(1)} %all_gather.16), channel_id=1, replica_groups=mesh['grp'=2,'row'=4,'col'=2,'cls'=2] {'row'}, dimensions={1}, use_global_device_ids=true | all-gather | bytes 81920 | tf_op jit(solution)/shard_map/all_gather | solution.py:104
  21.8 0.0 copy-done
  21.8 4.9 %all_gather.18 = bf16[256,256]{0,1:T(8,128)(2,1)S(1)} all-gather(bf16[256,128]{0,1:T(8,128)(2,1)S(1)} %bitcast.38), channel_id=1, replica_groups=mesh['grp'=2,'row'=4,'col'=2,'cls'=2] {'col'}, dimensions={1}, use_global_device_ids=true | all-gather | bytes 196608 | tf_op jit(solution)/shard_map/all_gather | solution.py:97
  26.7 15.9 %all_gather.19 = bf16[256,1024]{0,1:T(8,128)(2,1)S(1)} all-gather(bf16[256,256]{0,1:T(8,128)(2,1)S(1)} %all_gather.18), channel_id=1, replica_groups=mesh['grp'=2,'row'=4,'col'=2,'cls'=2] {'row'}, dimensions={1}, use_global_device_ids=true | all-gather | bytes 655360 | tf_op jit(solution)/shard_map/all_gather | solution.py:103
  42.6 0.2 multiply_reduce_fusion
  42.9 0.1 multiply_reduce_fusion.1
  43.0 0.0 copy-start.1
  43.0 0.6 %fusion.8 = f32[32,256]{1,0:T(8,128)S(1)} fusion(bf16[32,1024]{1,0:T(8,128)(2,1)S(1)} %all_gather.17, bf16[256,1024]{0,1:T(8,128)(2,1)S(1)} %all_gather.19, bf16[256,256]{1,0:T(8,128)(2,1)S(1)} %bitcast.37, f32[1024]{0:T(1024)S(1)} %multiply_reduce_fusion, f32[256]{0:T(256)S(1)} %bitcast.39, s32[1024]{0:T(1024)S(1)} %fusion.36, s32[256]{0:T(256)S(1)} %fusion.57), kind=kOutput, calls=%fused_computation.9 | convolution fusion | flops 153100288 | bytes 763904 | tf_op jit(solution)/shard_map/dot_general | solution.py:29
  43.6 0.1 copy-done.1
  43.7 0.2 fusion.21
  43.9 3.4 %psum.7 = f32[32,256]{1,0:T(8,128)S(1)} all-reduce(f32[32,256]{1,0:T(8,128)S(1)} %fusion.21), channel_id=1, replica_groups=mesh['grp'=2,'row'=4,'col'=2,'cls'=2] {'cls'}, use_global_device_ids=true, to_apply=%region_4.5 | all-reduce | flops 8192 | bytes 65536 | tf_op jit(solution)/shard_map/psum | solution.py:111
  47.3 0.1 select_reduce_fusion
  47.4 0.1 fusion.66
  47.5 0.6 %reshape.139 = bf16[16,2,128]{2,1,0:T(2,128)(2,1)} reshape(bf16[16,256]{1,0:T(8,128)(2,1)S(1)} %fusion.20) | data formatting | bytes 16384 | tf_op jit(solution)/shard_map/reshape | solution.py:115
  (6 shorter events, 0.0 us)
Async XLA Ops:
  0.0 2.2 %copy-start.2 = (f32[2,128]{1,0:T(2,128)S(1)}, f32[2,128]{1,0:T(2,128)}, u32[]{:S(2)}) copy-start(f32[2,128]{1,0:T(2,128)} %param.5) | copy-start | bytes 3076
  2.3 19.5 %copy-start = (bf16[2,128,256]{2,1,0:T(8,128)(2,1)S(1)}, bf16[2,128,256]{2,1,0:T(8,128)(2,1)}, u32[]{:S(2)}) copy-start(bf16[2,128,256]{2,1,0:T(8,128)(2,1)} %param.6) | copy-start | bytes 393220
  43.0 0.7 %copy-start.1 = (s32[32,32]{1,0:T(8,128)S(1)}, s32[32,32]{1,0:T(8,128)}, u32[]{:S(2)}) copy-start(s32[32,32]{1,0:T(8,128)} %param.7) | copy-start | bytes 12292
where the time goes:
time: 48.4 us; the launch traced here: 48.1 us
  blocking collectives  45.5 us (94%)
  local copies, waits for them, and re-layouts  0.88 us (2%)
  other arithmetic  0.87 us (2%)
  matrix products  0.77 us (2%)
    all_gather x1, blocking collectives, body(): lax.all_gather(band_feats, 'row', axis=1, tiled=True)  15.9 us
    all_gather x1, blocking collectives, body(): lax.all_gather(band_belief, 'row', axis=1, tiled=True)  14 us
    all_gather x1, blocking collectives, body(): lax.all_gather(key_belief, 'col', axis=1, tiled=True)  5.13 us
    all_gather x1, blocking collectives, body(): lax.all_gather(key_feats, 'col', axis=1, tiled=True)  4.93 us
    psum x1, blocking collectives, body(): pairwise = lax.psum(partial_value, 'cls')  3.41 us
    all_gather x1, blocking collectives, body(): whole_unary = lax.all_gather(unary_scores, 'cls', axis=0, tiled=True)  2.19 us

commit v1 on v0

v1 whole, which is shorter than its diff:
```python
import functools

import jax
import jax.numpy as jnp
from jax import lax
from jax.experimental import pallas as pl
from jax.experimental.pallas import tpu as pltpu
from jax.sharding import PartitionSpec as P

LIVE = 21

unit_scale = 1.0 / 64.0
masked_low = -1e30
MESH = pl.DeviceIdType.MESH
NT = (((1,), (1,)), ((), ()))


def class_softmax(logits, live_mask):
    class_top = jnp.max(jnp.where(live_mask, logits, masked_low), axis=0, keepdims=True)
    raised = jnp.where(live_mask, jnp.exp(logits - class_top), 0.0)
    return raised / jnp.sum(raised, axis=0, keepdims=True)


def spread_order(count):
    order = sorted(range(1, count), key=lambda o: (min(o, count - o), o))
    return order


def kernel(
    rows_n,
    cols_n,
    cls_n,
    unary_ref,
    conf_ref,
    feats_ref,
    compat_ref,
    out_ref,
    ubuf,
    kbuf,
    bbuf,
    qbuf,
    part,
    mbuf,
    fin,
    usend,
    urecv,
    ksend,
    krecv,
    bsend,
    brecv,
    qsend,
    qrecv,
    msend,
    mrecv,
):
    z = lax.axis_index("row")
    x = lax.axis_index("col")
    c = lax.axis_index("cls")
    share, row_count, col_count = unary_ref.shape
    depth = feats_ref.shape[2]
    classes = share * cls_n
    live_pad = mbuf.shape[-2]
    pixels = row_count * col_count
    half_rows = row_count // cls_n
    keys_local = half_rows * col_count

    def at_row(o):
        return {"row": lax.rem(z + o, rows_n)}

    def at_chip(xo, co):
        return {"col": lax.rem(x + xo, cols_n), "cls": lax.rem(c + co, cls_n)}

    returns = [(xo, co) for xo in range(cols_n) for co in range(cls_n) if xo or co]
    returns = sorted(returns, key=lambda p: (p[0] == 0, p))

    barrier = pltpu.get_barrier_semaphore()
    for o in range(1, rows_n):
        pl.semaphore_signal(barrier, inc=1, device_id=at_row(o), device_id_type=MESH)
    for xo, co in returns:
        pl.semaphore_signal(barrier, inc=1, device_id=at_chip(xo, co), device_id_type=MESH)
    pl.semaphore_wait(barrier, rows_n - 1 + len(returns))

    half = pl.ds(c * half_rows, half_rows)
    row_order = spread_order(rows_n)

    def row_copy(src, buf, o, ss, rs):
        return pltpu.make_async_remote_copy(
            src_ref=src,
            dst_ref=buf.at[o],
            send_sem=ss.at[o],
            recv_sem=rs.at[o],
            device_id=at_row(o),
            device_id_type=MESH,
        )

    ucopies = [
        pltpu.make_async_remote_copy(
            src_ref=unary_ref,
            dst_ref=ubuf.at[c],
            send_sem=usend.at[co],
            recv_sem=urecv.at[co],
            device_id=at_chip(0, co),
            device_id_type=MESH,
        )
        for co in range(1, cls_n)
    ]
    for copy in ucopies:
        copy.start()
    kcopies = {o: row_copy(feats_ref.at[half], kbuf, o, ksend, krecv) for o in row_order}
    for o in reversed(row_order):
        kcopies[o].start()
    qcopies = {
        xo: pltpu.make_async_remote_copy(
            src_ref=feats_ref,
            dst_ref=qbuf.at[xo],
            send_sem=qsend.at[xo],
            recv_sem=qrecv.at[xo],
            device_id=at_chip(xo, 0),
            device_id_type=MESH,
        )
        for xo in range(1, cols_n)
    }
    for xo in range(1, cols_n):
        qcopies[xo].start()

    ubuf[c] = unary_ref[...]
    live_mask = lax.broadcasted_iota(jnp.int32, (classes, 1), 0) < LIVE
    for copy in ucopies:
        copy.wait()

    def logits_of(r):
        conf = conf_ref[pl.ds(r, 1), :]
        scores = ubuf[:, :, pl.ds(r, 1), :].reshape(classes, col_count)
        return conf * (scores.astype(jnp.float32) * unit_scale)

    for r in range(half_rows):
        belief0 = class_softmax(logits_of(c * half_rows + r), live_mask)
        bbuf[0, :, r * col_count : (r + 1) * col_count] = belief0.astype(jnp.bfloat16)

    ones = jnp.ones((8, depth), jnp.bfloat16)
    scale = 2.0 / depth

    def query_of(xo):
        feats = feats_ref[...] if xo == 0 else qbuf[xo]
        feats = feats.reshape(pixels, depth)
        wide = feats.astype(jnp.float32)
        square = wide * wide
        high = square.astype(jnp.bfloat16)
        low = (square - high.astype(jnp.float32)).astype(jnp.bfloat16)
        norm = lax.dot_general(ones, high, NT, preferred_element_type=jnp.float32)
        norm = norm + lax.dot_general(ones, low, NT, preferred_element_type=jnp.float32)
        return feats, 2.0 - norm[:1] * scale

    def key_of(o):
        feats = feats_ref[half] if o == 0 else kbuf[o]
        feats = feats.reshape(keys_local, depth)
        wide = feats.astype(jnp.float32)
        return feats, 2.0 - jnp.sum(wide * wide, axis=1, keepdims=True) * scale

    def affinity(key, query, same):
        scores = lax.dot_general(key[0], query[0], NT, preferred_element_type=jnp.float32)
        value = jnp.exp(scores * (2.0 * scale) + (key[1] + query[1]))
        if same:
            place = c * keys_local + lax.broadcasted_iota(jnp.int32, (keys_local, pixels), 0)
            value = jnp.where(place == lax.broadcasted_iota(jnp.int32, (keys_local, pixels), 1), 0.0, value)
        return value.astype(jnp.bfloat16)

    def fold(belief, kern):
        return lax.dot_general(
            belief, kern, (((1,), (0,)), ((), ())), preferred_element_type=jnp.float32
        )

    own_query = query_of(0)
    own_key = key_of(0)
    first = affinity(own_key, own_query, True)

    bcopies = {o: row_copy(bbuf.at[0], bbuf, o, bsend, brecv) for o in row_order}
    for o in reversed(row_order):
        bcopies[o].start()

    own_belief = bbuf[0]
    sums = [fold(own_belief, first)]
    queries = [own_query]
    for xo in range(1, cols_n):
        qcopies[xo].wait_recv()
        queries.append(query_of(xo))
        sums.append(fold(own_belief, affinity(own_key, queries[xo], False)))
    for o in row_order:
        kcopies[o].wait_recv()
        key = key_of(o)
        kerns = [affinity(key, query, False) for query in queries]
        bcopies[o].wait_recv()
        belief = bbuf[o]
        sums = [total + fold(belief, kern) for total, kern in zip(sums, kerns)]

    for xo in range(cols_n):
        part[xo] = sums[xo][:live_pad]
    mcopies = {}
    for xo, co in returns:
        slot = xo * cls_n + co
        mcopies[slot] = pltpu.make_async_remote_copy(
            src_ref=part.at[xo],
            dst_ref=mbuf.at[slot],
            send_sem=msend.at[slot],
            recv_sem=mrecv.at[slot],
            device_id=at_chip(xo, co),
            device_id_type=MESH,
        )
        mcopies[slot].start()

    rows_i = lax.broadcasted_iota(jnp.int32, (live_pad, live_pad), 0)
    cols_i = lax.broadcasted_iota(jnp.int32, (live_pad, live_pad), 1)
    weight = jnp.where(rows_i == cols_i, 0.0, compat_ref[:live_pad, :live_pad].astype(jnp.float32))
    logits0 = jnp.concatenate([logits_of(r)[:live_pad] for r in range(row_count)], axis=1)
    message = sums[0][:live_pad]
    for slot in sorted(mcopies):
        mcopies[slot].wait_recv()
        message = message + mbuf[slot]
    message = message * (1.0 / (2.0 * pixels))
    pairwise = jnp.dot(
        weight, message, precision=lax.Precision.HIGHEST, preferred_element_type=jnp.float32
    )
    belief1 = class_softmax(logits0 - pairwise, live_mask[:live_pad])
    fin[:live_pad] = belief1
    if live_pad < classes:
        fin[live_pad:] = jnp.zeros((classes - live_pad, pixels), jnp.float32)
    out_ref[...] = fin[pl.ds(c * share, share), :].astype(jnp.bfloat16)

    for copies in (kcopies, bcopies, qcopies, mcopies):
        for copy in copies.values():
            copy.wait_send()


def body(unary_scores, confidence, features, compat_table):
    share, row_count, col_count = unary_scores.shape
    depth = features.shape[2]
    rows_n = lax.axis_size("row")
    cols_n = lax.axis_size("col")
    cls_n = lax.axis_size("cls")
    classes = share * cls_n
    live_pad = min(classes, -(-LIVE // 8) * 8)
    pixels = row_count * col_count
    half_rows = row_count // cls_n
    keys_local = half_rows * col_count
    dma = pltpu.SemaphoreType.DMA
    out = pl.pallas_call(
        functools.partial(kernel, rows_n, cols_n, cls_n),
        out_shape=jax.ShapeDtypeStruct((share, pixels), jnp.bfloat16),
        in_specs=[pl.BlockSpec(memory_space=pltpu.VMEM)] * 4,
        out_specs=pl.BlockSpec(memory_space=pltpu.VMEM),
        scratch_shapes=[
            pltpu.VMEM((cls_n, share, row_count, col_count), jnp.int32),
            pltpu.VMEM((rows_n, half_rows, col_count, depth), jnp.bfloat16),
            pltpu.VMEM((rows_n, classes, keys_local), jnp.bfloat16),
            pltpu.VMEM((cols_n, row_count, col_count, depth), jnp.bfloat16),
            pltpu.VMEM((cols_n, live_pad, pixels), jnp.float32),
            pltpu.VMEM((cols_n * cls_n, live_pad, pixels), jnp.float32),
            pltpu.VMEM((classes, pixels), jnp.float32),
            dma((cls_n,)),
            dma((cls_n,)),
            dma((rows_n,)),
            dma((rows_n,)),
            dma((rows_n,)),
            dma((rows_n,)),
            dma((cols_n,)),
            dma((cols_n,)),
            dma((cols_n * cls_n,)),
            dma((cols_n * cls_n,)),
        ],
        compiler_params=pltpu.CompilerParams(collective_id=0, has_side_effects=True),
    )(unary_scores, confidence, features, compat_table)
    return out.reshape(share, row_count, col_count)


def solution(mesh):
    in_specs = (
        P("cls", ("grp", "row"), "col"),
        P(("grp", "row"), "col"),
        P(("grp", "row"), "col", None),
        P(),
    )
    out_specs = P("cls", ("grp", "row"), "col")
    return jax.shard_map(body, mesh=mesh, in_specs=in_specs, out_specs=out_specs, check_vma=False)
```

time: 48.4 us -> 19.3 us (0.40)
  blocking collectives: 45.5 us -> 0 us
  Pallas kernels: 0 us -> 17.8 us
  other arithmetic: 0.87 us -> 0 us
  matrix products: 0.77 us -> 0 us
    all_gather x5 -> x0, blocking collectives: 42.1 us -> none  [the longest x1 15.9 us: body(): lax.all_gather(band_feats, 'row', axis=1, tiled=True)]
    pallas_call x0 -> x1, Pallas kernels: none -> 17.8 us  [body(): pl.pallas_call(functools.partial(kernel, rows_n, cols_n, cls_n), out_shap...]
    psum x1 -> x0, blocking collectives: 3.41 us -> none  [body(): pairwise = lax.psum(partial_value, 'cls')]
    dot_general x2 -> x0, matrix products: 0.77 us -> none  [the longest x1 0.61 us: add_block(): lax.dot_general(beliefs, kernel, (((1,), (1,)), ((), ())), preferred_elem...]
    reshape x2 -> x1, local copies, waits for them, and re-layouts: 0.7 us -> 1.3 us  [body(): return out.reshape(share, row_count, col_count)]
    reduce_sum x4 -> x0, other arithmetic: 0.52 us -> none  [the longest x1 0.21 us: add_block(): key_norm = jnp.sum(jnp.square(key_piece.astype(jnp.float32)), axis=0)]
where the time goes in v1:
time: 19.3 us; the launch traced here: 19.1 us
  Pallas kernels  17.8 us (92%)
  local copies, waits for them, and re-layouts  1.3 us (7%)
    pallas_call x1, Pallas kernels, body(): pl.pallas_call(functools.partial(kernel, rows_n, cols_n, cls_n), out_shap...  17.8 us
    reshape x1, local copies, waits for them, and re-layouts, body(): return out.reshape(share, row_count, col_count)  1.3 us

profile of v1, /device:TPU:0, one launch (start us, length us, event | category | flops | bytes accessed | tf_op | source)
XLA Modules:
  0.0 19.1 jit_solution(10388201158505291824)
XLA Ops:
  0.0 17.8 %shard_map.46 = bf16[16,256]{1,0:T(8,128)(2,1)} custom-call(s32[16,2,128]{2,1,0:T(2,128)} %unary_ref.1, f32[2,128]{1,0:T(2,128)} %conf_ref.1, bf16[2,128,256]{2,1,0:T(8,128)(2,1)} %feats_ref.1, s32[32,32]{1,0:T(8,128)} %compat_ref.1), custom_call_target="tpu_custom_call" | custom-call | tf_op jit(solution)/shard_map/pallas_call | solution.py:246
  17.8 1.3 %reshape.3 = bf16[16,2,128]{2,1,0:T(2,128)(2,1)} reshape(bf16[16,256]{1,0:T(8,128)(2,1)} %shard_map.46) | data formatting | bytes 16384 | tf_op jit(solution)/shard_map/reshape | solution.py:272

commit v2 on v1

v2 whole, which is shorter than its diff:
```python
import functools

import jax
import jax.numpy as jnp
from jax import lax
from jax.experimental import pallas as pl
from jax.experimental.pallas import tpu as pltpu
from jax.sharding import PartitionSpec as P

LIVE = 21

unit_scale = 1.0 / 64.0
masked_low = -1e30
MESH = pl.DeviceIdType.MESH
NT = (((1,), (1,)), ((), ()))


def class_softmax(logits, live_mask):
    class_top = jnp.max(jnp.where(live_mask, logits, masked_low), axis=0, keepdims=True)
    raised = jnp.where(live_mask, jnp.exp(logits - class_top), 0.0)
    return raised / jnp.sum(raised, axis=0, keepdims=True)


def split_rows(rows_n):
    low = max(d for d in range(1, rows_n + 1) if rows_n % d == 0 and d * d <= rows_n)
    return low, rows_n // low


def kernel(
    low_n,
    high_n,
    cols_n,
    cls_n,
    unary_hbm,
    conf_hbm,
    feats_hbm,
    compat_hbm,
    out_ref,
    conf_ref,
    feats_ref,
    compat_ref,
    ubuf,
    kbuf,
    bbuf,
    qbuf,
    part,
    mbuf,
    fin,
    obuf,
    load,
    usend,
    urecv,
    ksend,
    krecv,
    fsend,
    frecv,
    bsend,
    brecv,
    qsend,
    qrecv,
    msend,
    mrecv,
    osend,
    orecv,
):
    z = lax.axis_index("row")
    x = lax.axis_index("col")
    c = lax.axis_index("cls")
    z_low = lax.rem(z, low_n)
    z_high = z // low_n
    _, share, row_count, col_count = ubuf.shape
    depth = feats_ref.shape[2]
    classes = share * cls_n
    live_pad = mbuf.shape[-2]
    pixels = row_count * col_count
    half_rows = row_count // cls_n
    keys_local = half_rows * col_count

    def at_query(slot):
        lo, xo = slot // cols_n, slot % cols_n
        row = z_high * low_n + lax.rem(z_low + lo, low_n)
        return {"row": row, "col": lax.rem(x + xo, cols_n)}

    def from_query(slot):
        lo, xo = slot // cols_n, slot % cols_n
        row = z_high * low_n + lax.rem(z_low + (low_n - lo), low_n)
        return {"row": row, "col": lax.rem(x + (cols_n - xo), cols_n)}

    def at_key(ho):
        return {"row": lax.rem(z_high + ho, high_n) * low_n + z_low}

    def at_core(co):
        return {"cls": lax.rem(c + co, cls_n)}

    query_slots = range(1, low_n * cols_n)
    key_slots = range(1, high_n)
    core_slots = range(1, cls_n)

    barrier = pltpu.get_barrier_semaphore()
    targets = [at_key(o) for o in key_slots]
    targets += [at_query(s) for s in query_slots]
    targets += [at_core(o) for o in core_slots]
    for target in targets:
        pl.semaphore_signal(barrier, inc=1, device_id=target, device_id_type=MESH)

    loads = [
        pltpu.make_async_copy(src, dst, load.at[i])
        for i, (src, dst) in enumerate(
            (
                (feats_hbm, feats_ref),
                (unary_hbm, ubuf.at[c]),
                (conf_hbm, conf_ref),
                (compat_hbm, compat_ref),
            )
        )
    ]
    for copy in loads:
        copy.start()
    for copy in loads:
        copy.wait()
    pl.semaphore_wait(barrier, len(targets))

    def remote(src, dst, ss, rs, target):
        return pltpu.make_async_remote_copy(
            src_ref=src,
            dst_ref=dst,
            send_sem=ss,
            recv_sem=rs,
            device_id=target,
            device_id_type=MESH,
        )

    half = pl.ds(c * half_rows, half_rows)
    kcopies = {
        o: remote(feats_ref.at[half], kbuf.at[o, c], ksend.at[o], krecv.at[o], at_key(o))
        for o in key_slots
    }
    ucopies = {
        o: remote(ubuf.at[c], ubuf.at[c], usend.at[o], urecv.at[o], at_core(o))
        for o in core_slots
    }
    qcopies = {
        s: remote(feats_ref.at[half], qbuf.at[s], qsend.at[s], qrecv.at[s], at_query(s))
        for s in query_slots
    }
    for o in key_slots:
        kcopies[o].start()
    for o in core_slots:
        ucopies[o].start()
    for s in reversed(query_slots):
        qcopies[s].start()

    ones = jnp.ones((8, depth), jnp.bfloat16)
    scale = 2.0 / depth

    def query_of(feats):
        feats = feats.reshape(keys_local, depth)
        wide = feats.astype(jnp.float32)
        square = wide * wide
        high = square.astype(jnp.bfloat16)
        low = (square - high.astype(jnp.float32)).astype(jnp.bfloat16)
        norm = lax.dot_general(ones, high, NT, preferred_element_type=jnp.float32)
        norm = norm + lax.dot_general(ones, low, NT, preferred_element_type=jnp.float32)
        return feats, 2.0 - norm[:1] * scale

    def key_of(feats):
        feats = feats.reshape(-1, depth)
        wide = feats.astype(jnp.float32)
        return feats, 2.0 - jnp.sum(wide * wide, axis=1, keepdims=True) * scale

    def affinity(key, query, same):
        scores = lax.dot_general(key[0], query[0], NT, preferred_element_type=jnp.float32)
        value = jnp.exp(scores * (2.0 * scale) + (key[1] + query[1]))
        if same:
            key_place = lax.broadcasted_iota(jnp.int32, value.shape, 0)
            query_place = c * keys_local + lax.broadcasted_iota(jnp.int32, value.shape, 1)
            value = jnp.where(key_place == query_place, 0.0, value)
        return value.astype(jnp.bfloat16)

    def fold(belief, kern):
        return lax.dot_general(
            belief, kern, (((1,), (0,)), ((), ())), preferred_element_type=jnp.float32
        )

    live_mask = lax.broadcasted_iota(jnp.int32, (classes, 1), 0) < LIVE
    for o in core_slots:
        ucopies[o].wait()

    def logits_of(r):
        conf = conf_ref[pl.ds(r, 1), :]
        scores = ubuf[:, :, pl.ds(r, 1), :].reshape(classes, col_count)
        return conf * (scores.astype(jnp.float32) * unit_scale)

    for r in range(row_count):
        belief0 = class_softmax(logits_of(r), live_mask).astype(jnp.bfloat16)
        h, start = r // half_rows, r % half_rows * col_count
        bbuf[0, h, :, start : start + col_count] = belief0

    own_key = key_of(feats_ref[...])
    queries = [query_of(feats_ref[half])]
    first = affinity(own_key, queries[0], True)

    bcopies = {
        o: remote(bbuf.at[0], bbuf.at[o], bsend.at[o], brecv.at[o], at_key(o)) for o in key_slots
    }
    for o in key_slots:
        bcopies[o].start()

    own_belief = jnp.concatenate([bbuf[0, h] for h in range(cls_n)], axis=1)
    sums = [fold(own_belief, first)]
    for s in query_slots:
        qcopies[s].wait_recv()
        queries.append(query_of(qbuf[s]))
        sums.append(fold(own_belief, affinity(own_key, queries[s], False)))

    fcopies = {}
    for o in key_slots:
        kcopies[o].wait_recv()
        for co in core_slots:
            fcopies[o, co] = remote(
                kbuf.at[o, c], kbuf.at[o, c], fsend.at[o, co], frecv.at[o, co], at_core(co)
            )
            fcopies[o, co].start()
    for o in key_slots:
        bcopies[o].wait_recv()
    for co in range(cls_n):
        source = lax.rem(c + (cls_n - co), cls_n)
        for o in key_slots:
            if co:
                fcopies[o, co].wait_recv()
            key = key_of(kbuf[o, source])
            belief = bbuf[o, source]
            sums = [
                total + fold(belief, affinity(key, query, False))
                for total, query in zip(sums, queries)
            ]

    for s in query_slots:
        part[s] = sums[s][:live_pad]
    mcopies = {
        s: remote(part.at[s], mbuf.at[s], msend.at[s], mrecv.at[s], from_query(s))
        for s in query_slots
    }
    for s in reversed(query_slots):
        mcopies[s].start()

    rows_i = lax.broadcasted_iota(jnp.int32, (live_pad, live_pad), 0)
    cols_i = lax.broadcasted_iota(jnp.int32, (live_pad, live_pad), 1)
    weight = jnp.where(rows_i == cols_i, 0.0, compat_ref[:live_pad, :live_pad].astype(jnp.float32))
    logits0 = jnp.concatenate(
        [logits_of(c * half_rows + r)[:live_pad] for r in range(half_rows)], axis=1
    )
    message = sums[0][:live_pad]
    for s in query_slots:
        mcopies[s].wait_recv()
        message = message + mbuf[s]
    message = message * (1.0 / (2.0 * pixels))
    pairwise = jnp.dot(
        weight, message, precision=lax.Precision.HIGHEST, preferred_element_type=jnp.float32
    )
    belief1 = class_softmax(logits0 - pairwise, live_mask[:live_pad])
    if live_pad < classes:
        belief1 = jnp.concatenate(
            [belief1, jnp.zeros((classes - live_pad, keys_local), jnp.float32)], axis=0
        )
    fin[...] = belief1.astype(jnp.bfloat16).reshape(cls_n, share, keys_local)
    ocopies = {
        o: remote(
            fin.at[lax.rem(c + o, cls_n)], obuf.at[c], osend.at[o], orecv.at[o], at_core(o)
        )
        for o in core_slots
    }
    for o in core_slots:
        ocopies[o].start()
    obuf[c] = fin[c]
    for o in core_slots:
        ocopies[o].wait_recv()
    out_ref[...] = jnp.concatenate([obuf[h] for h in range(cls_n)], axis=1)

    for copies in (kcopies, bcopies, qcopies, fcopies, mcopies, ocopies):
        for copy in copies.values():
            copy.wait_send()


def body(unary_scores, confidence, features, compat_table):
    share, row_count, col_count = unary_scores.shape
    depth = features.shape[2]
    low_n, high_n = split_rows(lax.axis_size("row"))
    cols_n = lax.axis_size("col")
    cls_n = lax.axis_size("cls")
    classes = share * cls_n
    live_pad = min(classes, -(-LIVE // 8) * 8)
    pixels = row_count * col_count
    half_rows = row_count // cls_n
    keys_local = half_rows * col_count
    query_n = low_n * cols_n
    bf16, f32 = jnp.bfloat16, jnp.float32
    dma = pltpu.SemaphoreType.DMA
    out = pl.pallas_call(
        functools.partial(kernel, low_n, high_n, cols_n, cls_n),
        out_shape=jax.ShapeDtypeStruct((share, pixels), bf16),
        in_specs=[pl.BlockSpec(memory_space=pl.ANY)] * 4,
        out_specs=pl.BlockSpec(memory_space=pltpu.VMEM),
        scratch_shapes=[
            pltpu.VMEM(confidence.shape, confidence.dtype),
            pltpu.VMEM(features.shape, features.dtype),
            pltpu.VMEM(compat_table.shape, compat_table.dtype),
            pltpu.VMEM((cls_n, share, row_count, col_count), jnp.int32),
            pltpu.VMEM((high_n, cls_n, half_rows, col_count, depth), bf16),
            pltpu.VMEM((high_n, cls_n, classes, keys_local), bf16),
            pltpu.VMEM((query_n, half_rows, col_count, depth), bf16),
            pltpu.VMEM((query_n, live_pad, keys_local), f32),
            pltpu.VMEM((query_n, live_pad, keys_local), f32),
            pltpu.VMEM((cls_n, share, keys_local), bf16),
            pltpu.VMEM((cls_n, share, keys_local), bf16),
            dma((4,)),
            dma((cls_n,)),
            dma((cls_n,)),
            dma((high_n,)),
            dma((high_n,)),
            dma((high_n, cls_n)),
            dma((high_n, cls_n)),
            dma((high_n,)),
            dma((high_n,)),
            dma((query_n,)),
            dma((query_n,)),
            dma((query_n,)),
            dma((query_n,)),
            dma((cls_n,)),
            dma((cls_n,)),
        ],
        compiler_params=pltpu.CompilerParams(collective_id=0, has_side_effects=True),
    )(unary_scores, confidence, features, compat_table)
    return out.reshape(share, row_count, col_count)


def solution(mesh):
    in_specs = (
        P("cls", ("grp", "row"), "col"),
        P(("grp", "row"), "col"),
        P(("grp", "row"), "col", None),
        P(),
    )
    out_specs = P("cls", ("grp", "row"), "col")
    return jax.shard_map(body, mesh=mesh, in_specs=in_specs, out_specs=out_specs, check_vma=False)
```

time: 19.3 us -> 19 us (0.984)
  Pallas kernels: 17.8 us -> 17.5 us
    pallas_call x1, Pallas kernels: 17.8 us -> 17.5 us  [body(): pl.pallas_call(functools.partial(kernel, low_n, high_n, cols_n, cls_n), o...]
where the time goes in v2:
time: 19 us; the launch traced here: 18.8 us
  Pallas kernels  17.5 us (92%)
  local copies, waits for them, and re-layouts  1.3 us (7%)
    pallas_call x1, Pallas kernels, body(): pl.pallas_call(functools.partial(kernel, low_n, high_n, cols_n, cls_n), o...  17.5 us
    reshape x1, local copies, waits for them, and re-layouts, body(): return out.reshape(share, row_count, col_count)  1.3 us

profile of v2, /device:TPU:0, one launch (start us, length us, event | category | flops | bytes accessed | tf_op | source)
XLA Modules:
  0.0 18.8 jit_solution(14014735480367075041)
XLA Ops:
  0.0 17.5 %shard_map.46 = bf16[16,256]{1,0:T(8,128)(2,1)} custom-call(s32[16,2,128]{2,1,0:T(2,128)} %unary_hbm.1, f32[2,128]{1,0:T(2,128)} %conf_hbm.1, bf16[2,128,256]{2,1,0:T(8,128)(2,1)} %feats_hbm.1, s32[32,32]{1,0:T(8,128)} %compat_hbm.1), custom_call_target="tpu_custom_call" | custom-call | tf_op jit(solution)/shard_map/pallas_call | solution.py:299
  17.5 1.3 %reshape.3 = bf16[16,2,128]{2,1,0:T(2,128)(2,1)} reshape(bf16[16,256]{1,0:T(8,128)(2,1)} %shard_map.46) | data formatting | bytes 16384 | tf_op jit(solution)/shard_map/reshape | solution.py:334

commit v3 on v2

--- a/solution.py
+++ b/solution.py
@@ -147,7 +147,9 @@
         kcopies[o].start()
     for o in core_slots:
         ucopies[o].start()
-    for s in reversed(query_slots):
+    near = [s for s in query_slots if s < cols_n]
+    far = [s for s in query_slots if s >= cols_n]
+    for s in near:
         qcopies[s].start()
 
     ones = jnp.ones((8, depth), jnp.bfloat16)
@@ -196,16 +198,18 @@
         h, start = r // half_rows, r % half_rows * col_count
         bbuf[0, h, :, start : start + col_count] = belief0
 
-    own_key = key_of(feats_ref[...])
     queries = [query_of(feats_ref[half])]
-    first = affinity(own_key, queries[0], True)
 
     bcopies = {
         o: remote(bbuf.at[0], bbuf.at[o], bsend.at[o], brecv.at[o], at_key(o)) for o in key_slots
     }
     for o in key_slots:
         bcopies[o].start()
-
+    for s in reversed(far):
+        qcopies[s].start()
+
+    own_key = key_of(feats_ref[...])
+    first = affinity(own_key, queries[0], True)
     own_belief = jnp.concatenate([bbuf[0, h] for h in range(cls_n)], axis=1)
     sums = [fold(own_belief, first)]
     for s in query_slots:

time: 19 us -> 19.8 us (1.042)
  Pallas kernels: 17.5 us -> 18.3 us
    pallas_call x1, Pallas kernels: 17.5 us -> 18.3 us  [body(): pl.pallas_call(functools.partial(kernel, low_n, high_n, cols_n, cls_n), o...]
where the time goes in v3:
time: 19.8 us; the launch traced here: 19.6 us
  Pallas kernels  18.3 us (92%)
  local copies, waits for them, and re-layouts  1.3 us (7%)
    pallas_call x1, Pallas kernels, body(): pl.pallas_call(functools.partial(kernel, low_n, high_n, cols_n, cls_n), o...  18.3 us
    reshape x1, local copies, waits for them, and re-layouts, body(): return out.reshape(share, row_count, col_count)  1.3 us

profile of v3, /device:TPU:0, one launch (start us, length us, event | category | flops | bytes accessed | tf_op | source)
XLA Modules:
  0.0 19.6 jit_solution(5954434216419948034)
XLA Ops:
  0.0 18.3 %shard_map.46 = bf16[16,256]{1,0:T(8,128)(2,1)} custom-call(s32[16,2,128]{2,1,0:T(2,128)} %unary_hbm.1, f32[2,128]{1,0:T(2,128)} %conf_hbm.1, bf16[2,128,256]{2,1,0:T(8,128)(2,1)} %feats_hbm.1, s32[32,32]{1,0:T(8,128)} %compat_hbm.1), custom_call_target="tpu_custom_call" | custom-call | tf_op jit(solution)/shard_map/pallas_call | solution.py:303
  18.3 1.3 %reshape.3 = bf16[16,2,128]{2,1,0:T(2,128)(2,1)} reshape(bf16[16,256]{1,0:T(8,128)(2,1)} %shard_map.46) | data formatting | bytes 16384 | tf_op jit(solution)/shard_map/reshape | solution.py:338

commit v4 on v2

--- a/solution.py
+++ b/solution.py
@@ -154,7 +154,7 @@
     scale = 2.0 / depth
 
     def query_of(feats):
-        feats = feats.reshape(keys_local, depth)
+        feats = feats.reshape(-1, depth)
         wide = feats.astype(jnp.float32)
         square = wide * wide
         high = square.astype(jnp.bfloat16)
@@ -173,8 +173,9 @@
         value = jnp.exp(scores * (2.0 * scale) + (key[1] + query[1]))
         if same:
             key_place = lax.broadcasted_iota(jnp.int32, value.shape, 0)
-            query_place = c * keys_local + lax.broadcasted_iota(jnp.int32, value.shape, 1)
-            value = jnp.where(key_place == query_place, 0.0, value)
+            lane = lax.broadcasted_iota(jnp.int32, value.shape, 1)
+            mine = (lane < keys_local) & (key_place == c * keys_local + lane)
+            value = jnp.where(mine, 0.0, value)
         return value.astype(jnp.bfloat16)
 
     def fold(belief, kern):
@@ -197,8 +198,7 @@
         bbuf[0, h, :, start : start + col_count] = belief0
 
     own_key = key_of(feats_ref[...])
-    queries = [query_of(feats_ref[half])]
-    first = affinity(own_key, queries[0], True)
+    qbuf[0] = feats_ref[half]
 
     bcopies = {
         o: remote(bbuf.at[0], bbuf.at[o], bsend.at[o], brecv.at[o], at_key(o)) for o in key_slots
@@ -207,12 +207,15 @@
         bcopies[o].start()
 
     own_belief = jnp.concatenate([bbuf[0, h] for h in range(cls_n)], axis=1)
-    sums = [fold(own_belief, first)]
-    for s in query_slots:
-        qcopies[s].wait_recv()
-        queries.append(query_of(qbuf[s]))
-        sums.append(fold(own_belief, affinity(own_key, queries[s], False)))
-
+    queries, sums = [], []
+
+    def meet_group(lo):
+        for s in range(max(1, lo * cols_n), (lo + 1) * cols_n):
+            qcopies[s].wait_recv()
+        queries.append(query_of(qbuf[lo * cols_n : (lo + 1) * cols_n]))
+        sums.append(fold(own_belief, affinity(own_key, queries[lo], lo == 0)))
+
+    meet_group(0)
     fcopies = {}
     for o in key_slots:
         kcopies[o].wait_recv()
@@ -221,28 +224,32 @@
                 kbuf.at[o, c], kbuf.at[o, c], fsend.at[o, co], frecv.at[o, co], at_core(co)
             )
             fcopies[o, co].start()
+    for lo in range(1, low_n):
+        meet_group(lo)
+    keys, beliefs = [], []
     for o in key_slots:
         bcopies[o].wait_recv()
-    for co in range(cls_n):
-        source = lax.rem(c + (cls_n - co), cls_n)
-        for o in key_slots:
-            if co:
-                fcopies[o, co].wait_recv()
-            key = key_of(kbuf[o, source])
-            belief = bbuf[o, source]
-            sums = [
-                total + fold(belief, affinity(key, query, False))
-                for total, query in zip(sums, queries)
-            ]
-
-    for s in query_slots:
-        part[s] = sums[s][:live_pad]
+        for co in core_slots:
+            fcopies[o, co].wait_recv()
+        keys.append(key_of(kbuf[o]))
+        beliefs.append(jnp.concatenate([bbuf[o, h] for h in range(cls_n)], axis=1))
     mcopies = {
         s: remote(part.at[s], mbuf.at[s], msend.at[s], mrecv.at[s], from_query(s))
         for s in query_slots
     }
-    for s in reversed(query_slots):
-        mcopies[s].start()
+    own_sum = None
+    for lo in reversed(range(low_n)):
+        total = sums[lo]
+        for key, belief in zip(keys, beliefs):
+            total = total + fold(belief, affinity(key, queries[lo], False))
+        for xo in reversed(range(cols_n)):
+            s = lo * cols_n + xo
+            piece = total[:live_pad, xo * keys_local : (xo + 1) * keys_local]
+            if s == 0:
+                own_sum = piece
+            else:
+                part[s] = piece
+                mcopies[s].start()
 
     rows_i = lax.broadcasted_iota(jnp.int32, (live_pad, live_pad), 0)
     cols_i = lax.broadcasted_iota(jnp.int32, (live_pad, live_pad), 1)
@@ -250,7 +257,7 @@
     logits0 = jnp.concatenate(
         [logits_of(c * half_rows + r)[:live_pad] for r in range(half_rows)], axis=1
     )
-    message = sums[0][:live_pad]
+    message = own_sum
     for s in query_slots:
         mcopies[s].wait_recv()
         message = message + mbuf[s]

time: 19 us -> 18.4 us (0.968)
  Pallas kernels: 17.5 us -> 16.8 us
    pallas_call x1, Pallas kernels: 17.5 us -> 16.8 us  [body(): pl.pallas_call(functools.partial(kernel, low_n, high_n, cols_n, cls_n), o...]
where the time goes in v4:
time: 18.4 us; the launch traced here: 18.1 us
  Pallas kernels  16.8 us (91%)
  local copies, waits for them, and re-layouts  1.3 us (7%)
    pallas_call x1, Pallas kernels, body(): pl.pallas_call(functools.partial(kernel, low_n, high_n, cols_n, cls_n), o...  16.8 us
    reshape x1, local copies, waits for them, and re-layouts, body(): return out.reshape(share, row_count, col_count)  1.3 us

profile of v4, /device:TPU:0, one launch (start us, length us, event | category | flops | bytes accessed | tf_op | source)
XLA Modules:
  0.0 18.1 jit_solution(6794368009572454781)
XLA Ops:
  0.0 16.8 %shard_map.46 = bf16[16,256]{1,0:T(8,128)(2,1)} custom-call(s32[16,2,128]{2,1,0:T(2,128)} %unary_hbm.1, f32[2,128]{1,0:T(2,128)} %conf_hbm.1, bf16[2,128,256]{2,1,0:T(8,128)(2,1)} %feats_hbm.1, s32[32,32]{1,0:T(8,128)} %compat_hbm.1), custom_call_target="tpu_custom_call" | custom-call | tf_op jit(solution)/shard_map/pallas_call | solution.py:306
  16.8 1.3 %reshape.3 = bf16[16,2,128]{2,1,0:T(2,128)(2,1)} reshape(bf16[16,256]{1,0:T(8,128)(2,1)} %shard_map.46) | data formatting | bytes 16384 | tf_op jit(solution)/shard_map/reshape | solution.py:341

commit v5 on v4

--- a/solution.py
+++ b/solution.py
@@ -262,9 +262,12 @@
         mcopies[s].wait_recv()
         message = message + mbuf[s]
     message = message * (1.0 / (2.0 * pixels))
-    pairwise = jnp.dot(
-        weight, message, precision=lax.Precision.HIGHEST, preferred_element_type=jnp.float32
-    )
+    high = message.astype(jnp.bfloat16)
+    rest = message - high.astype(jnp.float32)
+    middle = rest.astype(jnp.bfloat16)
+    low = (rest - middle.astype(jnp.float32)).astype(jnp.bfloat16)
+    pieces = jnp.concatenate([high, middle, low], axis=0)
+    pairwise = fold(jnp.concatenate([weight.astype(jnp.bfloat16)] * 3, axis=1), pieces)
     belief1 = class_softmax(logits0 - pairwise, live_mask[:live_pad])
     if live_pad < classes:
         belief1 = jnp.concatenate(

time: 18.4 us -> 18.4 us (level)
  no operation moved by 1% of the time
where the time goes in v5:
time: 18.4 us; the launch traced here: 18.2 us
  Pallas kernels  16.8 us (91%)
  local copies, waits for them, and re-layouts  1.3 us (7%)
    pallas_call x1, Pallas kernels, body(): pl.pallas_call(functools.partial(kernel, low_n, high_n, cols_n, cls_n), o...  16.8 us
    reshape x1, local copies, waits for them, and re-layouts, body(): return out.reshape(share, row_count, col_count)  1.3 us

profile of v5, /device:TPU:0, one launch (start us, length us, event | category | flops | bytes accessed | tf_op | source)
XLA Modules:
  0.0 18.2 jit_solution(16420902967238679607)
XLA Ops:
  0.0 16.8 %shard_map.46 = bf16[16,256]{1,0:T(8,128)(2,1)} custom-call(s32[16,2,128]{2,1,0:T(2,128)} %unary_hbm.1, f32[2,128]{1,0:T(2,128)} %conf_hbm.1, bf16[2,128,256]{2,1,0:T(8,128)(2,1)} %feats_hbm.1, s32[32,32]{1,0:T(8,128)} %compat_hbm.1), custom_call_target="tpu_custom_call" | custom-call | tf_op jit(solution)/shard_map/pallas_call | solution.py:309
  16.9 1.3 %reshape.3 = bf16[16,2,128]{2,1,0:T(2,128)(2,1)} reshape(bf16[16,256]{1,0:T(8,128)(2,1)} %shard_map.46) | data formatting | bytes 16384 | tf_op jit(solution)/shard_map/reshape | solution.py:344
